TPU v7x, 128 devices: a whole 4x4x4 slice. The times are simulated.
128 devices in a mesh: irrep: 4 (over z), occ: 4 (over y), vir: 8 (over x, core).
Axes of the slice: x: 4, y: 4, z: 4, core: 2. Of those that a mesh axis runs over, the one named last changes fastest.
Arguments:
- amplitudes: bfloat16 [8, 320, 12288], P('irrep', None, ('occ', 'vir')), may hold values from -6 to 6
- ladder_ints: bfloat16 [8, 12288, 12288], P('irrep', ('occ', 'vir')), may hold values from -0.109375 to 0.109375
- hole_ints: bfloat16 [8, 320, 320], P('irrep'), may hold values from -0.3125 to 0.3125
- occ_energy: float32 [8, 320], P('irrep'), may hold values from -3 to -0.5
- vir_energy: float32 [8, 12288], P('irrep', ('occ', 'vir')), may hold values from 0.5 to 3
- occ_pairs: int32 [8], replicated, may hold values from 160 to 320, as said below
- vir_pairs: int32 [8], replicated, may hold values from 6144 to 12288, as said below
Outputs:
- updated: bfloat16 [8, 320, 12288], P('irrep', None, ('occ', 'vir'))
- residual_norm: float32 [8], P('irrep')
Inputs may be any that keep to these rules, and one draw needn't show every extreme that they name: `occ_pairs`: some block has exactly 320 live occupied pairs in every draw. `vir_pairs`: some block has exactly 12288 live virtual pairs in every draw.
All inputs are finite; a program needn't handle non-finite values.
Results may differ from a plain program's by a relative error of at most 0.001.
Values may be sent and summed in bfloat16 or wider, within the bound.
A program may use at most 128 MiB of HBM per device.

v0:
```python
import jax
import jax.numpy as jnp
from jax import lax
from jax.sharding import PartitionSpec as P

LEVEL_SHIFT = 0.5
EPSILON = 1e-06


def from_everyone(shard, axis):
    copies = jnp.broadcast_to(shard, (lax.axis_size(axis), *shard.shape))
    return lax.all_to_all(copies, axis, split_axis=0, concat_axis=0, tiled=True)


def of_everyone(shard, axis):
    return from_everyone(shard, axis).sum(axis=0)


def table_lookup(table, block_ids):
    entries = table.shape[0]
    match = jnp.arange(entries, dtype=jnp.int32)[None, :] == block_ids[:, None]
    return jnp.sum(jnp.where(match, table[None, :], 0), axis=1)


def body(amplitudes, ladder_ints, hole_ints, occ_energy, vir_energy, occ_pairs, vir_pairs):
    block_count, pair_rows, cols_here = amplitudes.shape
    vir_devices = lax.axis_size("vir")
    block_ids = lax.axis_index("irrep") * block_count + jnp.arange(block_count, dtype=jnp.int32)
    slot_index = lax.axis_index("occ") * vir_devices + lax.axis_index("vir")
    column_start = slot_index * cols_here
    occ_here = table_lookup(occ_pairs, block_ids)
    vir_here = table_lookup(vir_pairs, block_ids)
    row_index = jnp.arange(pair_rows, dtype=jnp.int32)
    col_index = column_start + jnp.arange(cols_here, dtype=jnp.int32)
    keep_mask = (row_index[None, :, None] < occ_here[:, None, None]) & (
        col_index[None, None, :] < vir_here[:, None, None]
    )
    masked = jnp.where(keep_mask, amplitudes, jnp.zeros((), amplitudes.dtype))
    product = jnp.einsum("hkc,hpk->chp", ladder_ints, masked, preferred_element_type=jnp.float32)
    summed = lax.psum_scatter(
        product.reshape(lax.axis_size(("occ", "vir")) * cols_here, block_count * pair_rows),
        ("occ", "vir"),
        scatter_dimension=0,
        tiled=True,
    )
    ladder_term = summed.reshape(cols_here, block_count, pair_rows).transpose(1, 2, 0)
    hole_term = jnp.einsum("hpr,hrq->hpq", hole_ints, masked, preferred_element_type=jnp.float32)
    wide = masked.astype(jnp.float32)
    denominator = vir_energy[:, None, :] - occ_energy[:, :, None]
    residual = jnp.where(
        keep_mask, ladder_term + hole_term + denominator * wide, jnp.zeros((), jnp.float32)
    )
    updated = (wide - residual / (denominator + LEVEL_SHIFT)).astype(jnp.bfloat16)
    squares = jnp.sum(residual * residual, axis=(1, 2))
    summed_squares = of_everyone(squares, ("occ", "vir"))
    pair_count = (occ_here * vir_here).astype(jnp.float32)
    residual_norm = jnp.sqrt(summed_squares / pair_count + EPSILON)
    return (updated, residual_norm)


def solution(mesh):
    in_specs = (
        P("irrep", None, ("occ", "vir")),
        P("irrep", ("occ", "vir"), None),
        P("irrep", None, None),
        P("irrep", None),
        P("irrep", ("occ", "vir")),
        P(),
        P(),
    )
    out_specs = (P("irrep", None, ("occ", "vir")), P("irrep"))
    return jax.shard_map(body, mesh=mesh, in_specs=in_specs, out_specs=out_specs, check_vma=False)
```

profile of v0, /device:TPU:1, one launch (start us, length us, event | category | flops | bytes accessed | tf_op | source)
XLA Modules:
  0.0 211.8 jit_solution(4515142815147542153)
XLA Ops:
  7.2 0.0 copy-start
  7.2 0.0 reduce-scatter.2.cloned.1.call-start
  7.2 0.9 select_reduce_fusion.1
  8.2 0.1 iota_compare_fusion
  8.2 0.1 broadcast_compare_fusion
  8.3 18.3 %fusion.5 = f32[2,320,12288]{2,1,0:T(8,128)} fusion(bf16[2,384,12288]{2,1,0:T(8,128)(2,1)} %param.8, bf16[2,320,384]{2,1,0:T(8,128)(2,1)} %param.7, pred[2,384]{1,0:T(4,128)(4,1)S(1)} %broadcast_compare_fusion, pred[2,320]{1,0:T(4,128)(4,1)S(1)} %iota_compare_fusion), kind=kOutput, calls=%fused_computation.11 | convolution fusion | flops 6040289280 | bytes 50824576 | tf_op jit(solution)/shard_map/hkc,hpk->chp/dot_general | solution.py:39
  26.6 0.0 copy-start.1
  26.6 0.0 copy-start.2
  26.6 0.0 copy-start.3
  26.6 0.0 reduce-scatter.2.cloned.1.call-update
  26.7 162.0 %reduce-scatter.2.cloned.1.call-done = f32[384,640]{0,1:T(8,128)} async-done(((f32[12288,640]{0,1:T(8,128)}), f32[384,640]{0,1:T(8,128)}) %reduce-scatter.2.cloned.1.call-update) | async-done | bytes 983056 | tf_op jit(solution)/shard_map/reduce_scatter | solution.py:40
  188.7 0.0 copy-done
  188.7 0.0 copy-done.1
  188.7 0.0 copy-done.2
  188.7 0.0 copy-done.3
  188.7 2.8 %multiply_reduce_fusion = (f32[2]{0:T(128)S(1)}, bf16[2,320,384]{2,1,0:T(8,128)(2,1)}) fusion(f32[2,320]{1,0:T(2,128)S(1)} %copy-done.2, f32[2,384]{1,0:T(2,128)S(1)} %copy-done.3, bf16[2,320,384]{2,1,0:T(8,128)(2,1)S(1)} %copy-done.1, pred[2,384]{1,0:T(4,128)(4,1)S(1)} %broadcast_compare_fusion, pred[2,320]{1,0:T(4,128)(4,1)S(1)} %iota_compare_fusion, ...), kind=kOutput, calls=%fused_computation.10 | convolution fusion | flops 161218560 | bytes 2382728 | tf_op jit(solution)/shard_map/hpr,hrq->hpq/dot_general | solution.py:47
  191.5 12.8 %all_to_all.6 = f32[32,1,2]{2,1,0:T(1,128)S(1)} all-to-all(f32[32,1,2]{2,1,0:T(1,128)S(1)} %broadcast_in_dim.46), channel_id=1, replica_groups=mesh['irrep'=4,'occ'=4,'vir'=8] {'occ','vir'}, dimensions={0} | all-to-all | bytes 512 | tf_op jit(solution)/shard_map/all_to_all | solution.py:12
  204.3 0.1 reduce_sum.39
  204.4 0.5 add_sqrt_fusion
  (3 shorter events, 0.0 us)
Async XLA Ops:
  7.2 181.5 %copy-start = (bf16[2,320,320]{2,1,0:T(8,128)(2,1)S(1)}, bf16[2,320,320]{2,1,0:T(8,128)(2,1)}, u32[]{:S(2)}) copy-start(bf16[2,320,320]{2,1,0:T(8,128)(2,1)} %param.9) | copy-start | bytes 1228804
  7.2 181.5 %reduce-scatter.2.cloned.1.call-start = ((), (), s32[]{:S(2)}) async-start(), calls=%async_computation.2 | async-start | bytes 32440320 | tf_op jit(solution)/shard_map/reduce_scatter | solution.py:40
  26.6 162.1 %copy-start.1 = (bf16[2,320,384]{2,1,0:T(8,128)(2,1)S(1)}, bf16[2,320,384]{2,1,0:T(8,128)(2,1)}, u32[]{:S(2)}) copy-start(bf16[2,320,384]{2,1,0:T(8,128)(2,1)} %param.7) | copy-start | bytes 1474564
  26.6 162.1 %copy-start.2 = (f32[2,320]{1,0:T(2,128)S(1)}, f32[2,320]{1,0:T(2,128)}, u32[]{:S(2)}) copy-start(f32[2,320]{1,0:T(2,128)} %param.10) | copy-start | bytes 7684
  26.6 162.1 %copy-start.3 = (f32[2,384]{1,0:T(2,128)S(1)}, f32[2,384]{1,0:T(2,128)}, u32[]{:S(2)}) copy-start(f32[2,384]{1,0:T(2,128)} %param.11) | copy-start | bytes 9220
Sparse Core Ops, SparseCore 0:
  26.8 161.8 reduce-scatter.1
where the time goes:
time: 212 us
  waiting for transfers between devices  162 us (76%)
  matrix products  21.1 us (10%)
  between operations  14.1 us (7%)
  blocking collectives  12.8 us (6%)
    reduce_scatter x1, waiting for transfers between devices, body(): lax.psum_scatter(product.reshape(lax.axis_size(('occ', 'vir')) * cols_her...  162 us
    dot_general x1, matrix products, body(): jnp.einsum('hkc,hpk->chp', ladder_ints, masked, preferred_element_type=jn...  18.3 us
    all_to_all x1, blocking collectives, from_everyone(): return lax.all_to_all(copies, axis, split_axis=0, concat_axis=0, tiled=True)  12.8 us
  transfers between devices with their start and end apart: 1, of which 1 were waited for; matrix products, arithmetic and copies ran while one was open for 0% of the time, Pallas kernels for 0%

commit v1 on v0

v1 whole, which is shorter than its diff:
```python
import functools

import jax
import jax.numpy as jnp
from jax import lax
from jax.experimental import pallas as pl
from jax.experimental.pallas import tpu as pltpu
from jax.sharding import PartitionSpec as P

LEVEL_SHIFT = 0.5
EPSILON = 1e-06
MESH = pl.DeviceIdType.MESH
REL = (2, 1, 3, 0)
STEPS_PER_OCTAVE = 128.0
CODE_RANGE = 32000.0
TINY = 1e-33


def kernel(
    dims,
    occ_pairs,
    vir_pairs,
    amp,
    hole,
    occ_e,
    vir_e,
    lad,
    out,
    norm_out,
    amp_peer,
    amat,
    ladbuf,
    part,
    gain,
    msg_out,
    msg_in,
    two_out,
    two_in,
    sq_mine,
    sq_all,
    amp_s,
    amp_r,
    lad_l,
    lad_s,
    lad_r,
    one_s,
    one_r,
    two_s,
    two_r,
    sq_s,
    sq_r,
):
    nx, ny = dims
    rows, cols = amp.shape[1:]
    half = rows // 2
    lanes = cols // 128
    groups = half // 16
    z, y, v = lax.axis_index("irrep"), lax.axis_index("occ"), lax.axis_index("vir")
    x, c = v // 2, v % 2
    peer = {"vir": x * 2 + (1 - c)}
    size = {0: nx, 1: ny}

    def shifted(axis, by):
        if axis == 0:
            return {"vir": ((x + by) % nx) * 2 + c}
        return {"occ": (y + by) % ny}

    def columns(b, s, t, core):
        i, j = (x, y) if b == 0 else (y, x)
        to_i, to_j = (i + REL[t]) % 4, (j + REL[s]) % 4
        to_x, to_y = (to_i, to_j) if b == 0 else (to_j, to_i)
        return pl.ds(pl.multiple_of(((to_y * nx + to_x) * 2 + core) * cols, 128), cols)

    for s in range(4):
        for t in range(4):
            for b in range(2):
                pltpu.make_async_copy(
                    lad.at[b, :, columns(b, s, t, c)],
                    ladbuf.at[b, s, pl.ds(0, cols), pl.ds(t * cols, cols)],
                    lad_l.at[b, s, t // 2],
                ).start()

    barrier = pltpu.get_barrier_semaphore()
    others = [(dy, dv) for dy in range(ny) for dv in range(2 * nx) if dy or dv]
    for dy, dv in others:
        pl.semaphore_signal(
            barrier, inc=1, device_id={"occ": (y + dy) % ny, "vir": (v + dv) % (2 * nx)}, device_id_type=MESH
        )
    pl.semaphore_wait(barrier, len(others))

    amp_copy = pltpu.make_async_remote_copy(amp, amp_peer, amp_s, amp_r, device_id=peer, device_id_type=MESH)
    amp_copy.start()
    for s in range(4):
        for t in range(4):
            for b in range(2):
                pltpu.make_async_remote_copy(
                    lad.at[b, :, columns(b, s, t, 1 - c)],
                    ladbuf.at[b, s, pl.ds(cols, cols), pl.ds(t * cols, cols)],
                    lad_s.at[b, s],
                    lad_r.at[b, s, t // 2],
                    device_id=peer,
                    device_id_type=MESH,
                ).start()

    def keep(b, core):
        n_occ, n_vir = occ_pairs[z * 2 + b], vir_pairs[z * 2 + b]
        first = ((y * nx + x) * 2 + core) * cols
        row = lax.broadcasted_iota(jnp.int32, (rows, cols), 0)
        col = lax.broadcasted_iota(jnp.int32, (rows, cols), 1) + first
        return (row < n_occ) & (col < n_vir)

    def masked(values, b, core):
        return jnp.where(keep(b, core), values.astype(jnp.float32), 0.0)

    def energy_gap(b):
        occ_col = jnp.broadcast_to(occ_e[b : b + 1, :], (128, rows)).T
        return vir_e[b : b + 1, :] - jnp.concatenate([occ_col] * lanes, axis=1)

    for b in range(2):
        wide = masked(amp[b], b, c)
        narrow = wide.astype(jnp.bfloat16)
        amat[b, :, pl.ds(0, cols)] = narrow
        gain[b] = jnp.dot(hole[b], narrow, preferred_element_type=jnp.float32) + energy_gap(b) * wide
    amp_copy.wait_recv()
    for b in range(2):
        amat[b, :, pl.ds(cols, cols)] = masked(amp_peer[b], b, 1 - c).astype(jnp.bfloat16)

    def encode(read, message):
        biggest = None
        for k in range(lanes):
            here = jnp.max(jnp.abs(read(k)).reshape(groups, 16, 128), axis=0)
            biggest = here if biggest is None else jnp.maximum(biggest, here)
        code = jnp.ceil(jnp.log2(jnp.maximum(biggest, TINY)) * STEPS_PER_OCTAVE) + 1.0
        up = jnp.exp2(code * (-1.0 / STEPS_PER_OCTAVE)) * CODE_RANGE
        for k in range(lanes):
            steps = jnp.round(read(k).reshape(groups, 16, 128) * up[None])
            message[pl.ds(k * groups, groups)] = steps.astype(jnp.int32).astype(jnp.int16)
        message[lanes * groups] = code.astype(jnp.int32).astype(jnp.int16)

    def decoded(message):
        code = message[lanes * groups].astype(jnp.int32).astype(jnp.float32)
        down = jnp.exp2(code * (1.0 / STEPS_PER_OCTAVE)) * (1.0 / CODE_RANGE)

        def read(k):
            steps = message[pl.ds(k * groups, groups)].astype(jnp.int32).astype(jnp.float32)
            return (steps * down[None]).reshape(half, 128)

        return read

    def piece(b, s, t, h):
        def ref(k):
            return part.at[b, s, pl.ds(h * half, half), pl.ds(t * cols + k * 128, 128)]

        return ref

    def values(ref):
        return lambda k: ref(k)[...]

    def add_into(ref, messages):
        reads = [decoded(m) for m in messages]
        for k in range(lanes):
            total = ref(k)[...]
            for read in reads:
                total = total + read(k)
            ref(k)[...] = total

    def send_one(b, s, m):
        return pltpu.make_async_remote_copy(
            msg_out.at[b, s, m],
            msg_in.at[b, s, m],
            one_s.at[b, s, m],
            one_r.at[b, s, m],
            device_id=shifted(b, 1 - 2 * (m % 2)),
            device_id_type=MESH,
        )

    def send_two(b, m):
        return pltpu.make_async_remote_copy(
            two_out.at[b, m],
            two_in.at[b, m],
            two_s.at[b, m],
            two_r.at[b, m],
            device_id=shifted(1 - b, 1 - 2 * (m % 2)),
            device_id_type=MESH,
        )

    def stage_a(s):
        for u in range(2):
            for b in range(2):
                width = pl.ds(u * 2 * cols, 2 * cols)
                mine = ladbuf.at[b, s, pl.ds(0, cols), width]
                pltpu.make_async_copy(mine, mine, lad_l.at[b, s, u]).wait()
                theirs = ladbuf.at[b, s, pl.ds(cols, cols), width]
                pltpu.make_async_copy(theirs, theirs, lad_r.at[b, s, u]).wait()
                part[b, s, :, width] = jnp.dot(
                    amat[b], ladbuf[b, s, :, width], preferred_element_type=jnp.float32
                )
                if u == 0:
                    encode(values(piece(b, s, 0, 0)), msg_out.at[b, s, 0])
                    encode(values(piece(b, s, 0, 1)), msg_out.at[b, s, 1])
                    send_one(b, s, 0).start()
                    send_one(b, s, 1).start()
                    encode(values(piece(b, s, 1, 1)), msg_out.at[b, s, 2])
                    send_one(b, s, 2).start()
                else:
                    encode(values(piece(b, s, 2, 0)), msg_out.at[b, s, 3])
                    send_one(b, s, 3).start()

    def stage_b(s):
        for b in range(2):
            for m, t in ((0, 1), (1, 2)):
                send_one(b, s, m).wait_recv()
                add_into(piece(b, s, t, m), [msg_in.at[b, s, m]])
                encode(values(piece(b, s, t, m)), msg_out.at[b, s, 4 + m])
                send_one(b, s, 4 + m).start()

    def stage_c(s):
        for b in range(2):
            for h, pair in enumerate(((4, 3), (2, 5))):
                for m in pair:
                    send_one(b, s, m).wait_recv()
                add_into(piece(b, s, 3, h), [msg_in.at[b, s, m] for m in pair])

    def two_first(s):
        for b in range(2):
            for m, (at, h) in enumerate(((0, 0), (0, 1), (1, 1), (2, 0))):
                if at == s:
                    encode(values(piece(b, s, 3, h)), two_out.at[b, m])
                    send_two(b, m).start()

    def two_second():
        for b in range(2):
            for m, s in ((0, 1), (1, 2)):
                send_two(b, m).wait_recv()
                add_into(piece(b, s, 3, m), [two_in.at[b, m]])
                encode(values(piece(b, s, 3, m)), two_out.at[b, 4 + m])
                send_two(b, 4 + m).start()

    def loop(t, carry):
        @pl.when(t < 4)
        def _():
            stage_a(t)

        @pl.when((t > 0) & (t < 5))
        def _():
            stage_b(t - 1)

        @pl.when(t > 1)
        def _():
            stage_c(t - 2)

        for s in range(3):

            @pl.when(t == s + 2)
            def _():
                two_first(s)

        @pl.when(t == 4)
        def _():
            two_second()

        return carry

    lax.fori_loop(0, 6, loop, 0)

    for b in range(2):
        for h, pair in enumerate(((4, 3), (2, 5))):
            for m in pair:
                send_two(b, m).wait_recv()
            add_into(piece(b, 3, 3, h), [two_in.at[b, m] for m in pair])
        wide = amat[b, :, pl.ds(0, cols)].astype(jnp.float32)
        ladder = part[b, 3, :, pl.ds(3 * cols, cols)]
        residual = jnp.where(keep(b, c), ladder + gain[b], 0.0)
        out[b] = (wide - residual / (energy_gap(b) + LEVEL_SHIFT)).astype(jnp.bfloat16)
        lane_sums = jnp.sum(residual * residual, axis=0, keepdims=True)
        total = lane_sums[:, :128]
        for k in range(1, lanes):
            total = total + lane_sums[:, k * 128 : (k + 1) * 128]
        sq_mine[pl.ds(b, 1), :] = total

    def send_sq(dy, dv, slot):
        return pltpu.make_async_remote_copy(
            sq_mine,
            sq_all.at[slot],
            sq_s,
            sq_r,
            device_id={"occ": (y + dy) % ny, "vir": (v + dv) % (2 * nx)},
            device_id_type=MESH,
        )

    for slot, (dy, dv) in enumerate(others):
        send_sq(dy, dv, slot).start()
    pltpu.make_async_copy(sq_all, sq_all, sq_r).wait()
    total = jnp.sum(sq_all[...], axis=0) + sq_mine[...]
    total = jnp.broadcast_to(jnp.sum(total, axis=1, keepdims=True), (2, 128))
    counts = [(occ_pairs[z * 2 + b] * vir_pairs[z * 2 + b]).astype(jnp.float32) for b in range(2)]
    block = lax.broadcasted_iota(jnp.int32, (2, 128), 0)
    norm_out[...] = jnp.sqrt(total / jnp.where(block == 0, counts[0], counts[1]) + EPSILON)

    pltpu.make_async_copy(sq_all, sq_all, sq_s).wait()
    amp_copy.wait_send()

    def drain(s, carry):
        for b in range(2):
            theirs = ladbuf.at[b, s, pl.ds(cols, cols), :]
            pltpu.make_async_copy(theirs, theirs, lad_s.at[b, s]).wait()
            for m in range(6):
                send_one(b, s, m).wait_send()
        return carry

    lax.fori_loop(0, 4, drain, 0)
    for b in range(2):
        for m in range(6):
            send_two(b, m).wait_send()


def body(amplitudes, ladder_ints, hole_ints, occ_energy, vir_energy, occ_pairs, vir_pairs):
    blocks, rows, cols = amplitudes.shape
    ny, nv = lax.axis_size("occ"), lax.axis_size("vir")
    nx = nv // 2
    tiles = (rows // 32) * (cols // 128) + 1
    smem, vmem = pl.BlockSpec(memory_space=pltpu.SMEM), pl.BlockSpec(memory_space=pltpu.VMEM)
    dma = pltpu.SemaphoreType.DMA
    updated, norm = pl.pallas_call(
        functools.partial(kernel, (nx, ny)),
        out_shape=(
            jax.ShapeDtypeStruct((blocks, rows, cols), jnp.bfloat16),
            jax.ShapeDtypeStruct((2, 128), jnp.float32),
        ),
        in_specs=[smem, smem, vmem, vmem, vmem, vmem, pl.BlockSpec(memory_space=pl.ANY)],
        out_specs=(vmem, vmem),
        scratch_shapes=[
            pltpu.VMEM((2, rows, cols), jnp.bfloat16),
            pltpu.VMEM((2, rows, 2 * cols), jnp.bfloat16),
            pltpu.VMEM((2, 4, 2 * cols, 4 * cols), jnp.bfloat16),
            pltpu.VMEM((2, 4, rows, 4 * cols), jnp.float32),
            pltpu.VMEM((2, rows, cols), jnp.float32),
            pltpu.VMEM((2, 4, 6, tiles, 16, 128), jnp.int16),
            pltpu.VMEM((2, 4, 6, tiles, 16, 128), jnp.int16),
            pltpu.VMEM((2, 6, tiles, 16, 128), jnp.int16),
            pltpu.VMEM((2, 6, tiles, 16, 128), jnp.int16),
            pltpu.VMEM((2, 128), jnp.float32),
            pltpu.VMEM((ny * nv - 1, 2, 128), jnp.float32),
            dma,
            dma,
            dma((2, 4, 2)),
            dma((2, 4)),
            dma((2, 4, 2)),
            dma((2, 4, 6)),
            dma((2, 4, 6)),
            dma((2, 6)),
            dma((2, 6)),
            dma,
            dma,
        ],
        compiler_params=pltpu.CompilerParams(
            collective_id=0, has_side_effects=True, vmem_limit_bytes=66_000_000
        ),
    )(occ_pairs, vir_pairs, amplitudes, hole_ints, occ_energy, vir_energy, ladder_ints)
    return updated, norm[:, 0]


def solution(mesh):
    in_specs = (
        P("irrep", None, ("occ", "vir")),
        P("irrep", ("occ", "vir"), None),
        P("irrep", None, None),
        P("irrep", None),
        P("irrep", ("occ", "vir")),
        P(),
        P(),
    )
    out_specs = (P("irrep", None, ("occ", "vir")), P("irrep"))
    return jax.shard_map(body, mesh=mesh, in_specs=in_specs, out_specs=out_specs, check_vma=False)
```

time: 212 us -> 67 us (0.32)
  waiting for transfers between devices: 162 us -> 0 us
  Pallas kernels: 0 us -> 63 us
  matrix products: 21.1 us -> 0 us
  between operations: 14.1 us -> 0.64 us
  blocking collectives: 12.8 us -> 0 us
  local copies, waits for them, and re-layouts: 0.03 us -> 3.14 us
    reduce_scatter x1 -> x0, waiting for transfers between devices: 162 us -> none  [body(): lax.psum_scatter(product.reshape(lax.axis_size(('occ', 'vir')) * cols_her...]
    pallas_call x0 -> x1, Pallas kernels: none -> 63 us  [body(): pl.pallas_call(functools.partial(kernel, (nx, ny)), out_shape=(jax.ShapeD...]
    dot_general x2 -> x0, matrix products: 21.1 us -> none  [the longest x1 18.3 us: body(): jnp.einsum('hkc,hpk->chp', ladder_ints, masked, preferred_element_type=jn...]
    all_to_all x1 -> x0, blocking collectives: 12.8 us -> none  [from_everyone(): return lax.all_to_all(copies, axis, split_axis=0, concat_axis=0, tiled=True)]
  transfers between devices with their start and end apart: 1 -> 0, of which waited for: 1 -> 0; matrix products, arithmetic and copies ran while one was open for 0% -> 0% of each run, Pallas kernels for 0% -> 0%
where the time goes in v1:
time: 67 us; the launch traced here: 66.8 us
  Pallas kernels  63 us (94%)
  local copies, waits for them, and re-layouts  3.14 us (5%)
    pallas_call x1, Pallas kernels, body(): pl.pallas_call(functools.partial(kernel, (nx, ny)), out_shape=(jax.ShapeD...  63 us
    unnamed x1, local copies, waits for them, and re-layouts  1.86 us

profile of v1, /device:TPU:1, one launch (start us, length us, event | category | flops | bytes accessed | tf_op | source)
XLA Modules:
  0.0 66.8 jit_solution(4499349652322858276)
XLA Ops:
  0.6 63.0 %shard_map.86 = (bf16[2,320,384]{2,1,0:T(8,128)(2,1)}, f32[2,128]{1,0:T(2,128)}) custom-call(s32[8]{0:T(128)} %occ_pairs.1, s32[8]{0:T(128)} %vir_pairs.1, bf16[2,320,384]{2,1,0:T(8,128)(2,1)} %amp.1, bf16[2,320,320]{2,1,0:T(8,128)(2,1)} %hole.1, f32[2,320]{1,0:T(2,128)} %occ_e.1, f32[2,384]{1,0:T(2,128)} %vir_e.1, bf16[2,384,12288]{2,1,0:T(8,128)(2,1)} %lad.1), custom_call_target="tpu_custom_call" | custom-call | tf_op jit(solution)/shard_map/pallas_call | solution.py:324
  63.7 1.3 %slice_reduce_fusion = f32[2]{0:T(128)} fusion(f32[2,128]{1,0:T(2,128)} %get-tuple-element.5), kind=kLoop, calls=%fused_computation | loop fusion | bytes 16 | tf_op jit(solution)/shard_map/slice | solution.py:360
  65.0 1.9 %copy.10 = bf16[2,320,384]{2,1,0:T(8,128)(2,1)} copy(bf16[2,320,384]{2,1,0:T(8,128)(2,1)} %get-tuple-element.8) | data formatting | bytes 983040

commit v2 on v1

v2 whole, which is shorter than its diff:
```python
import functools

import jax
import jax.numpy as jnp
from jax import lax
from jax.experimental import pallas as pl
from jax.experimental.pallas import tpu as pltpu
from jax.sharding import PartitionSpec as P

LEVEL_SHIFT = 0.5
EPSILON = 1e-06
MESH = pl.DeviceIdType.MESH
SPLIT = (slice(0, 1), slice(1, 4))
ORDER = ((0, 0), (1, 0), (0, 1), (2, 0), (1, 1), (3, 0), (2, 1), (3, 1))
REL = (2, 1, 3, 0)
STEPS_PER_OCTAVE = 128.0
CODE_RANGE = 32000.0
TINY = 1e-33


def kernel(
    dims,
    occ_pairs_hbm,
    vir_pairs_hbm,
    amp_hbm,
    hole_hbm,
    occ_e_hbm,
    vir_e_hbm,
    lad,
    out,
    norm_out,
    occ_pairs,
    vir_pairs,
    amp,
    hole,
    occ_e,
    vir_e,
    amp_peer,
    first,
    amat,
    ladbuf,
    part,
    gain,
    msg_out,
    msg_in,
    two_out,
    two_in,
    sq_mine,
    sq_all,
    load_s,
    first_s,
    amp_s,
    amp_r,
    lad_s,
    lad_r,
    one_s,
    one_r,
    two_s,
    two_r,
    sq_s,
    sq_r,
):
    nx, ny = dims
    rows, cols = amp.shape[1:]
    half = rows // 2
    lanes = cols // 128
    groups = half // 8
    data = lanes * groups
    z, y, v = lax.axis_index("irrep"), lax.axis_index("occ"), lax.axis_index("vir")
    x, c = v // 2, v % 2
    peer = {"vir": x * 2 + (1 - c)}
    size = {0: nx, 1: ny}

    def shifted(axis, by):
        if axis == 0:
            return {"vir": ((x + by) % nx) * 2 + c}
        return {"occ": (y + by) % ny}

    def columns(b, s, t, core):
        i, j = (x, y) if b == 0 else (y, x)
        to_i, to_j = (i + REL[t]) % 4, (j + REL[s]) % 4
        to_x, to_y = (to_i, to_j) if b == 0 else (to_j, to_i)
        return pl.ds(pl.multiple_of(((to_y * nx + to_x) * 2 + core) * cols, 128), cols)

    barrier = pltpu.get_barrier_semaphore()
    neighbours = [peer] + [shifted(axis, by) for axis in (0, 1) for by in (1, -1)]
    for device in neighbours:
        pl.semaphore_signal(barrier, inc=1, device_id=device, device_id_type=MESH)

    def load(n):
        src, dst = (
            (amp_hbm, amp),
            (occ_pairs_hbm, occ_pairs),
            (vir_pairs_hbm, vir_pairs),
            (occ_e_hbm, occ_e),
            (vir_e_hbm, vir_e),
            (hole_hbm, hole),
        )[n]
        return pltpu.make_async_copy(src, dst, load_s.at[n])

    def load_first(b):
        return pltpu.make_async_copy(lad.at[b, :, columns(b, 0, 0, 1 - c)], first.at[b], first_s.at[b])

    def load_ladder(g):
        s, u = ORDER[g]
        for b in range(2):
            for t in range(4)[SPLIT[u]]:
                pltpu.make_async_copy(
                    lad.at[b, :, columns(b, s, t, c)],
                    ladbuf.at[b, s, pl.ds(0, cols), pl.ds(t * cols, cols)],
                    lad_r.at[b, s, u],
                ).start()

    def swap_ladder(g):
        s, u = ORDER[g]
        for b in range(2):
            if g == 0:
                swap_amp(b).start()
            for t in range(4)[SPLIT[u]]:
                pltpu.make_async_remote_copy(
                    first.at[b] if g == 0 else lad.at[b, :, columns(b, s, t, 1 - c)],
                    ladbuf.at[b, s, pl.ds(cols, cols), pl.ds(t * cols, cols)],
                    lad_s.at[s],
                    lad_r.at[b, s, u],
                    device_id=peer,
                    device_id_type=MESH,
                ).start()

    def swap_amp(b):
        return pltpu.make_async_remote_copy(
            amp.at[b], amp_peer.at[b], amp_s, amp_r.at[b], device_id=peer, device_id_type=MESH
        )

    load(0).start()
    for b in range(2):
        load_first(b).start()
    for n in (1, 2):
        load(n).start()
    load_ladder(0)
    pl.semaphore_wait(barrier, len(neighbours))
    load(0).wait()
    for b in range(2):
        load_first(b).wait()
    swap_ladder(0)
    load_ladder(1)
    swap_ladder(1)
    load_ladder(2)
    for n in (3, 4, 5):
        load(n).start()
    for n in (1, 2):
        load(n).wait()

    def keep(b, core):
        n_occ, n_vir = occ_pairs[z * 2 + b], vir_pairs[z * 2 + b]
        first = ((y * nx + x) * 2 + core) * cols
        row = lax.broadcasted_iota(jnp.int32, (rows, cols), 0)
        col = lax.broadcasted_iota(jnp.int32, (rows, cols), 1) + first
        return (row < n_occ) & (col < n_vir)

    def masked(values, b, core):
        return jnp.where(keep(b, core), values.astype(jnp.float32), 0.0)

    def energy_gap(b):
        occ_col = jnp.broadcast_to(occ_e[b : b + 1, :], (128, rows)).T
        return vir_e[b : b + 1, :] - jnp.concatenate([occ_col] * lanes, axis=1)

    def amplitudes(b):
        amat[b, :, pl.ds(0, cols)] = masked(amp[b], b, c).astype(jnp.bfloat16)
        swap_amp(b).wait_recv()
        amat[b, :, pl.ds(cols, cols)] = masked(amp_peer[b], b, 1 - c).astype(jnp.bfloat16)

    def local_terms(b):
        narrow = amat[b, :, pl.ds(0, cols)]
        hole_term = jnp.dot(hole[b], narrow, preferred_element_type=jnp.float32)
        gain[b] = hole_term + energy_gap(b) * narrow.astype(jnp.float32)

    def encode(ref, message):
        biggest = None
        for k in range(lanes):
            here = jnp.max(jnp.abs(ref(k)[...]).reshape(groups, 8, 128), axis=0)
            biggest = here if biggest is None else jnp.maximum(biggest, here)
        code = jnp.ceil(jnp.log2(jnp.maximum(biggest, TINY)) * STEPS_PER_OCTAVE) + 1.0
        up = jnp.exp2(code * (-1.0 / STEPS_PER_OCTAVE)) * CODE_RANGE
        for k in range(lanes):
            steps = jnp.round(ref(k)[...].reshape(groups, 8, 128) * up[None])
            message[pl.ds(k * groups, groups)] = steps.astype(jnp.int32).astype(jnp.int16)
        message[data] = code.astype(jnp.int32).astype(jnp.int16)

    def decoded(message):
        code = message[data].astype(jnp.int32).astype(jnp.float32)
        down = jnp.exp2(code * (1.0 / STEPS_PER_OCTAVE)) * (1.0 / CODE_RANGE)

        def read(k):
            steps = message[pl.ds(k * groups, groups)].astype(jnp.int32).astype(jnp.float32)
            return (steps * down[None]).reshape(half, 128)

        return read

    def piece(b, s, t, h):
        def ref(k):
            return part.at[b, s, pl.ds(h * half, half), pl.ds(t * cols + k * 128, 128)]

        return ref

    def add_into(ref, messages):
        reads = [decoded(m) for m in messages]
        for k in range(lanes):
            total = ref(k)[...]
            for read in reads:
                total = total + read(k)
            ref(k)[...] = total

    def send_one(b, s, m):
        return pltpu.make_async_remote_copy(
            msg_out.at[b, s, m],
            msg_in.at[b, s, m],
            one_s.at[s],
            one_r.at[b, s, min(m, 2)],
            device_id=shifted(b, 1 - 2 * (m % 2)),
            device_id_type=MESH,
        )

    def send_two(b, m):
        return pltpu.make_async_remote_copy(
            two_out.at[b, m],
            two_in.at[b, m],
            two_s,
            two_r.at[b, min(m, 2)],
            device_id=shifted(1 - b, 1 - 2 * (m % 2)),
            device_id_type=MESH,
        )

    def products(b, s, u):
        ts = range(4)[SPLIT[u]]
        width = pl.ds(ts[0] * cols, len(ts) * cols)
        both = ladbuf.at[b, s, :, width]
        pltpu.make_async_copy(both, both, lad_r.at[b, s, u]).wait()
        part[b, s, :, width] = jnp.dot(amat[b], ladbuf[b, s, :, width], preferred_element_type=jnp.float32)

    def emit(b, s, u):
        for d in range(2):
            t, h = (0, d) if u == 0 else (1 + d, 1 - d)
            encode(piece(b, s, t, h), msg_out.at[b, s, 2 * u + d])
            send_one(b, s, 2 * u + d).start()

    def stage_a(s, u):
        for b in range(2):
            if s == 0 and u == 0:
                amplitudes(b)
            products(b, s, u)
            emit(b, s, u)

    def stage_b(s):
        for b in range(2):
            for d in range(2):
                send_one(b, s, d).wait_recv()
                add_into(piece(b, s, 1 + d, d), [msg_in.at[b, s, d]])
                encode(piece(b, s, 1 + d, d), msg_out.at[b, s, 4 + d])
                send_one(b, s, 4 + d).start()

    def stage_c(s):
        for b in range(2):
            rest = msg_in.at[b, s, pl.ds(2, 4)]
            pltpu.make_async_copy(rest, rest, one_r.at[b, s, 2]).wait()
            for d in range(2):
                add_into(piece(b, s, 3, d), [msg_in.at[b, s, m] for m in (4 + d, 3 - d)])

    def two_first(m):
        at, h = ((0, 0), (0, 1), (1, 1), (2, 0))[m]
        for b in range(2):
            encode(piece(b, at, 3, h), two_out.at[b, m])
            send_two(b, m).start()

    def two_second(m):
        for b in range(2):
            send_two(b, m).wait_recv()
            add_into(piece(b, 1 + m, 3, m), [two_in.at[b, m]])
            encode(piece(b, 1 + m, 3, m), two_out.at[b, 4 + m])
            send_two(b, 4 + m).start()

    stage_a(0, 0)
    swap_ladder(2)
    load_ladder(3)
    stage_a(1, 0)
    stage_a(0, 1)
    swap_ladder(3)
    load_ladder(4)
    stage_b(0)
    swap_ladder(4)
    load_ladder(5)
    stage_a(2, 0)
    stage_a(1, 1)
    swap_ladder(5)
    load_ladder(6)
    swap_ladder(6)
    load_ladder(7)
    stage_b(1)
    stage_c(0)
    two_first(0)
    two_first(1)
    swap_ladder(7)
    stage_a(3, 0)
    stage_a(2, 1)
    stage_b(2)
    stage_c(1)
    two_first(2)
    for n in (3, 4, 5):
        load(n).wait()
    for b in range(2):
        products(b, 3, 1)
        local_terms(b)
    stage_b(3)
    two_second(0)
    for b in range(2):
        emit(b, 3, 1)
    stage_c(2)
    two_first(3)
    two_second(1)
    stage_c(3)

    for b in range(2):
        rest = two_in.at[b, pl.ds(2, 4)]
        pltpu.make_async_copy(rest, rest, two_r.at[b, 2]).wait()
        for h, pair in enumerate(((4, 3), (2, 5))):
            add_into(piece(b, 3, 3, h), [two_in.at[b, m] for m in pair])
        ladder = part[b, 3, :, pl.ds(3 * cols, cols)]
        residual = jnp.where(keep(b, c), ladder + gain[b], 0.0)
        gain[b] = residual
        lane_sums = jnp.sum(residual * residual, axis=0, keepdims=True)
        total = lane_sums[:, :128]
        for k in range(1, lanes):
            total = total + lane_sums[:, k * 128 : (k + 1) * 128]
        sq_mine[pl.ds(b, 1), :] = total

    others = [(dy, dv) for dy in range(ny) for dv in range(2 * nx) if dy or dv]

    def send_sq(dy, dv, slot):
        return pltpu.make_async_remote_copy(
            sq_mine,
            sq_all.at[slot],
            sq_s,
            sq_r,
            device_id={"occ": (y + dy) % ny, "vir": (v + dv) % (2 * nx)},
            device_id_type=MESH,
        )

    for slot, (dy, dv) in enumerate(others):
        send_sq(dy, dv, slot).start()
    for b in range(2):
        wide = amat[b, :, pl.ds(0, cols)].astype(jnp.float32)
        out[b] = (wide - gain[b] / (energy_gap(b) + LEVEL_SHIFT)).astype(jnp.bfloat16)
    pltpu.make_async_copy(sq_all, sq_all, sq_r).wait()
    total = jnp.sum(sq_all[...], axis=0) + sq_mine[...]
    total = jnp.broadcast_to(jnp.sum(total, axis=1, keepdims=True), (2, 128))
    counts = [(occ_pairs[z * 2 + b] * vir_pairs[z * 2 + b]).astype(jnp.float32) for b in range(2)]
    block = lax.broadcasted_iota(jnp.int32, (2, 128), 0)
    norm_out[...] = jnp.sqrt(total / jnp.where(block == 0, counts[0], counts[1]) + EPSILON)

    pltpu.make_async_copy(sq_all, sq_all, sq_s).wait()
    pltpu.make_async_copy(amp_peer, amp_peer, amp_s).wait()
    pltpu.make_async_copy(two_out, two_out, two_s).wait()
    for s in range(4):
        theirs = ladbuf.at[:, s, pl.ds(cols, cols), :]
        pltpu.make_async_copy(theirs, theirs, lad_s.at[s]).wait()
        pltpu.make_async_copy(msg_out.at[:, s], msg_out.at[:, s], one_s.at[s]).wait()


def body(amplitudes, ladder_ints, hole_ints, occ_energy, vir_energy, occ_pairs, vir_pairs):
    blocks, rows, cols = amplitudes.shape
    ny, nv = lax.axis_size("occ"), lax.axis_size("vir")
    nx = nv // 2
    tiles = (rows // 16) * (cols // 128) + 1
    vmem = pl.BlockSpec(memory_space=pltpu.VMEM)
    dma = pltpu.SemaphoreType.DMA
    updated, norm = pl.pallas_call(
        functools.partial(kernel, (nx, ny)),
        out_shape=(
            jax.ShapeDtypeStruct((blocks, rows, cols), jnp.bfloat16),
            jax.ShapeDtypeStruct((2, 128), jnp.float32),
        ),
        in_specs=[pl.BlockSpec(memory_space=pltpu.HBM)] * 7,
        out_specs=(vmem, vmem),
        scratch_shapes=[
            pltpu.SMEM(occ_pairs.shape, jnp.int32),
            pltpu.SMEM(vir_pairs.shape, jnp.int32),
            pltpu.VMEM(amplitudes.shape, amplitudes.dtype),
            pltpu.VMEM(hole_ints.shape, hole_ints.dtype),
            pltpu.VMEM(occ_energy.shape, jnp.float32),
            pltpu.VMEM(vir_energy.shape, jnp.float32),
            pltpu.VMEM((2, rows, cols), jnp.bfloat16),
            pltpu.VMEM((2, cols, cols), jnp.bfloat16),
            pltpu.VMEM((2, rows, 2 * cols), jnp.bfloat16),
            pltpu.VMEM((2, 4, 2 * cols, 4 * cols), jnp.bfloat16),
            pltpu.VMEM((2, 4, rows, 4 * cols), jnp.float32),
            pltpu.VMEM((2, rows, cols), jnp.float32),
            pltpu.VMEM((2, 4, 6, tiles, 8, 128), jnp.int16),
            pltpu.VMEM((2, 4, 6, tiles, 8, 128), jnp.int16),
            pltpu.VMEM((2, 6, tiles, 8, 128), jnp.int16),
            pltpu.VMEM((2, 6, tiles, 8, 128), jnp.int16),
            pltpu.VMEM((2, 128), jnp.float32),
            pltpu.VMEM((ny * nv - 1, 2, 128), jnp.float32),
            dma((6,)),
            dma((2,)),
            dma,
            dma((2,)),
            dma((4,)),
            dma((2, 4, 2)),
            dma((4,)),
            dma((2, 4, 3)),
            dma,
            dma((2, 3)),
            dma,
            dma,
        ],
        compiler_params=pltpu.CompilerParams(
            collective_id=0, has_side_effects=True, vmem_limit_bytes=55_500_000
        ),
    )(
        *(
            pltpu.with_memory_space_constraint(array, pltpu.HBM)
            for array in (occ_pairs, vir_pairs, amplitudes, hole_ints, occ_energy, vir_energy, ladder_ints)
        )
    )
    return updated, norm[:, 0]


def solution(mesh):
    in_specs = (
        P("irrep", None, ("occ", "vir")),
        P("irrep", ("occ", "vir"), None),
        P("irrep", None, None),
        P("irrep", None),
        P("irrep", ("occ", "vir")),
        P(),
        P(),
    )
    out_specs = (P("irrep", None, ("occ", "vir")), P("irrep"))
    return jax.shard_map(body, mesh=mesh, in_specs=in_specs, out_specs=out_specs, check_vma=False)
```

time: 67 us -> 58.8 us (0.88)
  Pallas kernels: 63 us -> 56.7 us
  local copies, waits for them, and re-layouts: 3.14 us -> 1.4 us
    pallas_call x1, Pallas kernels: 63 us -> 56.7 us  [body(): pl.pallas_call(functools.partial(kernel, (nx, ny)), out_shape=(jax.ShapeD...]
    unnamed x1, local copies, waits for them, and re-layouts: 1.86 us -> 0.78 us
where the time goes in v2:
time: 58.8 us; the launch traced here: 58.7 us
  Pallas kernels  56.7 us (96%)
  local copies, waits for them, and re-layouts  1.4 us (2%)
  between operations  0.64 us (1%)
    pallas_call x1, Pallas kernels, body(): pl.pallas_call(functools.partial(kernel, (nx, ny)), out_shape=(jax.ShapeD...  56.7 us

profile of v2, /device:TPU:1, one launch (start us, length us, event | category | flops | bytes accessed | tf_op | source)
XLA Modules:
  0.0 58.7 jit_solution(17669874830264046969)
XLA Ops:
  0.6 56.7 %shard_map.86 = (bf16[2,320,384]{2,1,0:T(8,128)(2,1)S(1)}, f32[2,128]{1,0:T(2,128)S(1)}) custom-call(s32[8]{0:T(128)} %occ_pairs_hbm.1, s32[8]{0:T(128)} %vir_pairs_hbm.1, bf16[2,320,384]{2,1,0:T(8,128)(2,1)} %amp_hbm.1, bf16[2,320,320]{2,1,0:T(8,128)(2,1)} %hole_hbm.1, f32[2,320]{1,0:T(2,128)} %occ_e_hbm.1, f32[2,384]{1,0:T(2,128)} %vir_e_hbm.1, ...), custom_call_target="tpu_custom_call" | custom-call | tf_op jit(solution)/shard_map/pallas_call | solution.py:375
  57.3 0.6 %slice_reduce_fusion = f32[2]{0:T(128)} fusion(f32[2,128]{1,0:T(2,128)S(1)} %get-tuple-element.5), kind=kLoop, calls=%fused_computation | loop fusion | bytes 16 | tf_op jit(solution)/shard_map/slice | solution.py:424
  57.9 0.8 %copy.10 = bf16[2,320,384]{2,1,0:T(8,128)(2,1)} copy(bf16[2,320,384]{2,1,0:T(8,128)(2,1)S(1)} %get-tuple-element.8) | data formatting | bytes 983040

commit v3 on v2

v3 whole, which is shorter than its diff:
```python
import functools

import jax
import jax.numpy as jnp
from jax import lax
from jax.experimental import pallas as pl
from jax.experimental.pallas import tpu as pltpu
from jax.sharding import PartitionSpec as P

LEVEL_SHIFT = 0.5
EPSILON = 1e-06
MESH = pl.DeviceIdType.MESH
LEAD = 128
SPLIT = (slice(0, 1), slice(1, 4))
ORDER = ((0, 0), (1, 0), (2, 0), (0, 1), (3, 0), (1, 1), (2, 1), (3, 1))
REL = (2, 1, 3, 0)
STEPS_PER_OCTAVE = 128.0
CODE_RANGE = 32000.0
TINY = 1e-33


def kernel(
    dims,
    occ_pairs_hbm,
    vir_pairs_hbm,
    amp_hbm,
    hole_hbm,
    occ_e_hbm,
    vir_e_hbm,
    lad,
    out,
    norm_out,
    occ_pairs,
    vir_pairs,
    amp,
    hole,
    occ_e,
    vir_e,
    amp_peer,
    first,
    far_out,
    far_in,
    rear_out,
    rear_in,
    amat,
    ladbuf,
    part,
    gain,
    gap_of,
    msg_out,
    msg_in,
    two_out,
    two_in,
    sq_mine,
    sq_all,
    load_s,
    first_s,
    mine_s,
    late_r,
    far_s,
    far_r,
    amp_s,
    amp_r,
    lad_s,
    lad_r,
    one_s,
    one_r,
    two_s,
    last_r,
    two_r,
    sq_s,
    sq_r,
):
    nx, ny = dims
    rows, cols = amp.shape[1:]
    half = rows // 2
    lanes = cols // 128
    groups = half // 8
    whole = range(lanes)
    parts = (whole[: LEAD // 128], whole[LEAD // 128 :])
    z, y, v = lax.axis_index("irrep"), lax.axis_index("occ"), lax.axis_index("vir")
    x, c = v // 2, v % 2
    peer = {"vir": x * 2 + (1 - c)}
    size = {0: nx, 1: ny}

    def shifted(axis, by):
        if axis == 0:
            return {"vir": ((x + by) % nx) * 2 + c}
        return {"occ": (y + by) % ny}

    def columns(b, s, t, core):
        i, j = (x, y) if b == 0 else (y, x)
        to_i, to_j = (i + REL[t]) % 4, (j + REL[s]) % 4
        to_x, to_y = (to_i, to_j) if b == 0 else (to_j, to_i)
        return pl.ds(pl.multiple_of(((to_y * nx + to_x) * 2 + core) * cols, 128), cols)

    def load(n):
        src, dst = (
            (amp_hbm.at[0], amp.at[0]),
            (amp_hbm.at[1], amp.at[1]),
            (occ_pairs_hbm, occ_pairs),
            (vir_pairs_hbm, vir_pairs),
            (occ_e_hbm, occ_e),
            (vir_e_hbm, vir_e),
            (hole_hbm, hole),
        )[n]
        return pltpu.make_async_copy(src, dst, load_s.at[n])

    def load_first(b, n):
        width = LEAD if n == 0 else cols - LEAD
        at = pl.multiple_of(columns(b, 0, 0, 1 - c).start + n * LEAD, 128)
        return pltpu.make_async_copy(
            lad.at[b, :, pl.ds(at, width)], first.at[b, :, pl.ds(n * LEAD, width)], first_s.at[b, n]
        )

    def load_ladder(g):
        s, u = ORDER[g]
        for b in range(2):
            for t in range(4)[SPLIT[u]]:
                pltpu.make_async_copy(
                    lad.at[b, :, columns(b, s, t, c)],
                    ladbuf.at[b, s, pl.ds(0, cols), pl.ds(t * cols, cols)],
                    mine_s.at[b] if g == 0 else lad_r.at[b, 2 * s + u],
                ).start()

    def swap_first(b, part_no):
        where = pl.ds(LEAD * part_no, (cols - LEAD) * part_no + LEAD * (1 - part_no))
        return pltpu.make_async_remote_copy(
            first.at[b, :, where],
            ladbuf.at[b, 0, pl.ds(cols, cols), where],
            lad_s.at[0],
            lad_r.at[b, 0] if part_no == 0 else late_r.at[b],
            device_id=peer,
            device_id_type=MESH,
        )

    def swap_ladder(g):
        s, u = ORDER[g]
        for b in range(2):
            for t in range(4)[SPLIT[u]]:
                pltpu.make_async_remote_copy(
                    lad.at[b, :, columns(b, s, t, 1 - c)],
                    ladbuf.at[b, s, pl.ds(cols, cols), pl.ds(t * cols, cols)],
                    lad_s.at[s],
                    lad_r.at[b, 2 * s + u],
                    device_id=peer,
                    device_id_type=MESH,
                ).start()

    def swap_amp(b):
        return pltpu.make_async_remote_copy(
            amp.at[b], amp_peer.at[b], amp_s, amp_r.at[b], device_id=peer, device_id_type=MESH
        )

    for b in range(2):
        load(b).start()
    barrier = pltpu.get_barrier_semaphore()
    neighbours = [peer] + [shifted(axis, by) for axis in (0, 1) for by in (1, -1)]
    for device in neighbours:
        pl.semaphore_signal(barrier, inc=1, device_id=device, device_id_type=MESH)
    for n in range(2):
        for b in range(2):
            load_first(b, n).start()
    for n in (2, 3):
        load(n).start()
    load_ladder(0)
    pl.semaphore_wait(barrier, len(neighbours))
    for b in range(2):
        load(b).wait()
        swap_amp(b).start()
    for n in range(2):
        for b in range(2):
            load_first(b, n).wait()
            swap_first(b, n).start()
    load_ladder(1)
    swap_ladder(1)
    load_ladder(2)
    for n in (4, 5, 6):
        load(n).start()
    for n in (2, 3):
        load(n).wait()

    def keep(b, core, h=None):
        n_occ, n_vir = occ_pairs[z * 2 + b], vir_pairs[z * 2 + b]
        shape = (rows if h is None else half, cols)
        row = lax.broadcasted_iota(jnp.int32, shape, 0) + (0 if h is None else h * half)
        col = lax.broadcasted_iota(jnp.int32, shape, 1) + ((y * nx + x) * 2 + core) * cols
        return (row < n_occ) & (col < n_vir)

    def masked(values, b, core):
        return jnp.where(keep(b, core), values.astype(jnp.float32), 0.0)

    def local_terms(b):
        narrow = amat[b, :, pl.ds(0, cols)]
        occ_col = jnp.broadcast_to(occ_e[b : b + 1, :], (128, rows)).T
        gap = vir_e[b : b + 1, :] - jnp.concatenate([occ_col] * lanes, axis=1)
        gap_of[b] = gap
        hole_term = jnp.dot(hole[b], narrow, preferred_element_type=jnp.float32)
        gain[b] = hole_term + gap * narrow.astype(jnp.float32)

    def update(h):
        some = pl.ds(h * half, half)
        for b in range(2):
            wide = amat[b, some, pl.ds(0, cols)].astype(jnp.float32)
            out[b, some, :] = (wide - gain[b, some, :] / (gap_of[b, some, :] + LEVEL_SHIFT)).astype(jnp.bfloat16)

    def amplitudes(b):
        amat[b, :, pl.ds(0, cols)] = masked(amp[b], b, c).astype(jnp.bfloat16)
        swap_amp(b).wait_recv()
        amat[b, :, pl.ds(cols, cols)] = masked(amp_peer[b], b, 1 - c).astype(jnp.bfloat16)

    def encode(ref, message, blocks):
        biggest = None
        for k in blocks:
            here = jnp.max(jnp.abs(ref(k)[...]).reshape(groups, 8, 128), axis=0)
            biggest = here if biggest is None else jnp.maximum(biggest, here)
        code = jnp.ceil(jnp.log2(jnp.maximum(biggest, TINY)) * STEPS_PER_OCTAVE) + 1.0
        up = jnp.exp2(code * (-1.0 / STEPS_PER_OCTAVE)) * CODE_RANGE
        for n, k in enumerate(blocks):
            steps = jnp.round(ref(k)[...].reshape(groups, 8, 128) * up[None])
            message[pl.ds(n * groups, groups)] = steps.astype(jnp.int32).astype(jnp.int16)
        message[len(blocks) * groups] = code.astype(jnp.int32).astype(jnp.int16)

    def decoded(message, blocks):
        code = message[len(blocks) * groups].astype(jnp.int32).astype(jnp.float32)
        down = jnp.exp2(code * (1.0 / STEPS_PER_OCTAVE)) * (1.0 / CODE_RANGE)

        def read(k):
            at = pl.ds((k - blocks[0]) * groups, groups)
            steps = message[at].astype(jnp.int32).astype(jnp.float32)
            return (steps * down[None]).reshape(half, 128)

        return read

    def piece(b, s, t, h):
        def ref(k):
            return part.at[b, s, pl.ds(h * half, half), pl.ds(t * cols + k * 128, 128)]

        return ref

    def add_into(ref, messages, blocks):
        reads = [decoded(m, blocks) for m in messages]
        for k in blocks:
            total = ref(k)[...]
            for read in reads:
                total = total + read(k)
            ref(k)[...] = total

    def send_one(b, s, m):
        return pltpu.make_async_remote_copy(
            msg_out.at[b, s, m],
            msg_in.at[b, s, m],
            one_s.at[s],
            last_r.at[b, m - 2] if s == 3 and m > 1 else one_r.at[b, 2 * s - 2 + m if m < 2 else 6 + s],
            device_id=shifted(b, 1 - 2 * (m % 2)),
            device_id_type=MESH,
        )

    def send_two(b, m):
        return pltpu.make_async_remote_copy(
            two_out.at[b, m],
            two_in.at[b, m],
            two_s,
            two_r.at[b, m],
            device_id=shifted(1 - b, 1 - 2 * (m % 2)),
            device_id_type=MESH,
        )

    def send_far(b, d, n):
        return pltpu.make_async_remote_copy(
            (far_out, rear_out)[n].at[b, d],
            (far_in, rear_in)[n].at[b, d],
            far_s.at[n],
            far_r.at[b, d, n],
            device_id=shifted(b, 1 - 2 * d),
            device_id_type=MESH,
        )

    def stage_first():
        for b in range(2):
            amplitudes(b)
        for n in range(2):
            for b in range(2):
                own = ladbuf.at[b, 0, pl.ds(0, cols), pl.ds(0, cols)]
                if n == 0:
                    pltpu.make_async_copy(own, own, mine_s.at[b]).wait()
                swap_first(b, n).wait_recv()
                width = pl.ds(n * LEAD, len(parts[n]) * 128)
                part[b, 0, :, width] = jnp.dot(
                    amat[b], ladbuf[b, 0, :, width], preferred_element_type=jnp.float32
                )
                for d in range(2):
                    encode(piece(b, 0, 0, d), (far_out, rear_out)[n].at[b, d], parts[n])
                    send_far(b, d, n).start()

    def products(b, s, u):
        ts = range(4)[SPLIT[u]]
        width = pl.ds(ts[0] * cols, len(ts) * cols)
        both = ladbuf.at[b, s, :, width]
        pltpu.make_async_copy(both, both, lad_r.at[b, 2 * s + u]).wait()
        part[b, s, :, width] = jnp.dot(amat[b], ladbuf[b, s, :, width], preferred_element_type=jnp.float32)

    def emit(b, s, u):
        for d in range(2):
            t, h = (0, d) if u == 0 else (1 + d, 1 - d)
            encode(piece(b, s, t, h), msg_out.at[b, s, 2 * u + d], whole)
            send_one(b, s, 2 * u + d).start()

    def stage_a(s, u):
        for b in range(2):
            products(b, s, u)
            emit(b, s, u)

    def stage_b(s):
        for b in range(2):
            for d in range(2):
                if s == 0:
                    for n in range(2):
                        send_far(b, d, n).wait_recv()
                        add_into(piece(b, s, 1 + d, d), [(far_in, rear_in)[n].at[b, d]], parts[n])
                else:
                    send_one(b, s, d).wait_recv()
                    add_into(piece(b, s, 1 + d, d), [msg_in.at[b, s, d]], whole)
                encode(piece(b, s, 1 + d, d), msg_out.at[b, s, 4 + d], whole)
                send_one(b, s, 4 + d).start()

    def stage_c(s):
        for b in range(2):
            rest = msg_in.at[b, s, pl.ds(2, 4)]
            pltpu.make_async_copy(rest, rest, one_r.at[b, 6 + s]).wait()
            for d in range(2):
                add_into(piece(b, s, 3, d), [msg_in.at[b, s, m] for m in (4 + d, 3 - d)], whole)

    def two_first(m):
        at, h = ((0, 0), (0, 1), (1, 1), (2, 0))[m]
        for b in range(2):
            encode(piece(b, at, 3, h), two_out.at[b, m], whole)
            send_two(b, m).start()

    def two_second(m):
        for b in range(2):
            send_two(b, m).wait_recv()
            add_into(piece(b, 1 + m, 3, m), [two_in.at[b, m]], whole)
            encode(piece(b, 1 + m, 3, m), two_out.at[b, 4 + m], whole)
            send_two(b, 4 + m).start()

    stage_first()
    swap_ladder(2)
    load_ladder(3)
    stage_a(1, 0)
    swap_ladder(3)
    load_ladder(4)
    stage_a(2, 0)
    swap_ladder(4)
    load_ladder(5)
    stage_a(0, 1)
    stage_b(0)
    swap_ladder(5)
    load_ladder(6)
    stage_a(3, 0)
    stage_a(1, 1)
    swap_ladder(6)
    load_ladder(7)
    stage_b(1)
    stage_c(0)
    two_first(0)
    two_first(1)
    swap_ladder(7)
    stage_a(2, 1)
    stage_b(2)
    stage_c(1)
    two_first(2)
    for n in (4, 5, 6):
        load(n).wait()
    for b in range(2):
        products(b, 3, 1)
        local_terms(b)
    stage_b(3)
    two_second(0)
    for b in range(2):
        emit(b, 3, 1)
    stage_c(2)
    two_first(3)
    two_second(1)

    totals = [None, None]
    def add_one(b, h, m):
        send_one(b, 3, m).wait_recv()
        add_into(piece(b, 3, 3, h), [msg_in.at[b, 3, m]], whole)

    def add_two(b, h, m):
        send_two(b, m).wait_recv()
        add_into(piece(b, 3, 3, h), [two_in.at[b, m]], whole)

    def finish(b, h):
        some = pl.ds(h * half, half)
        ladder = part[b, 3, some, pl.ds(3 * cols, cols)]
        residual = jnp.where(keep(b, c, h), ladder + gain[b, some, :], 0.0)
        gain[b, some, :] = residual
        lane_sums = jnp.sum(residual * residual, axis=0, keepdims=True)
        for k in whole:
            here = lane_sums[:, k * 128 : (k + 1) * 128]
            totals[b] = here if totals[b] is None else totals[b] + here

    for b in range(2):
        add_one(b, 0, 4)
        add_two(b, 0, 4)
    for b in range(2):
        add_one(b, 1, 5)
        add_two(b, 1, 2)
    for b in range(2):
        add_one(b, 0, 3)
        add_two(b, 0, 3)
        finish(b, 0)
    update(0)
    for b in range(2):
        add_one(b, 1, 2)
        add_two(b, 1, 5)
        finish(b, 1)
    for b in range(2):
        sq_mine[pl.ds(b, 1), :] = totals[b]

    others = [(dy, dv) for dy in range(ny) for dv in range(2 * nx) if dy or dv]
    others.sort(key=lambda o: -(min(o[0], ny - o[0]) + min(o[1] // 2, nx - o[1] // 2)))

    def send_sq(dy, dv, slot):
        return pltpu.make_async_remote_copy(
            sq_mine,
            sq_all.at[slot],
            sq_s,
            sq_r,
            device_id={"occ": (y + dy) % ny, "vir": (v + dv) % (2 * nx)},
            device_id_type=MESH,
        )

    for slot, (dy, dv) in enumerate(others):
        send_sq(dy, dv, slot).start()
    update(1)
    pltpu.make_async_copy(amp_peer, amp_peer, amp_s).wait()
    pltpu.make_async_copy(two_out, two_out, two_s).wait()
    for n, lot in enumerate((far_out, rear_out)):
        pltpu.make_async_copy(lot, lot, far_s.at[n]).wait()
    for s in range(4):
        theirs = ladbuf.at[:, s, pl.ds(cols, cols), :]
        pltpu.make_async_copy(theirs, theirs, lad_s.at[s]).wait()
        sent = msg_out.at[:, s] if s else msg_out.at[:, s, pl.ds(2, 4)]
        pltpu.make_async_copy(sent, sent, one_s.at[s]).wait()
    pltpu.make_async_copy(sq_all, sq_all, sq_s).wait()
    pltpu.make_async_copy(sq_all, sq_all, sq_r).wait()
    total = jnp.sum(sq_all[...], axis=0) + sq_mine[...]
    total = jnp.broadcast_to(jnp.sum(total, axis=1, keepdims=True), (2, 128))
    counts = [(occ_pairs[z * 2 + b] * vir_pairs[z * 2 + b]).astype(jnp.float32) for b in range(2)]
    block = lax.broadcasted_iota(jnp.int32, (2, 128), 0)
    norm = jnp.sqrt(total / jnp.where(block == 0, counts[0], counts[1]) + EPSILON)
    lane = lax.broadcasted_iota(jnp.int32, (1, 128), 1)
    norm_out[...] = jnp.where(lane == 0, norm[:1, :], norm[1:, :]).reshape(128)


def body(amplitudes, ladder_ints, hole_ints, occ_energy, vir_energy, occ_pairs, vir_pairs):
    blocks, rows, cols = amplitudes.shape
    ny, nv = lax.axis_size("occ"), lax.axis_size("vir")
    nx = nv // 2
    tiles = (rows // 16) * (cols // 128) + 1
    lead = (rows // 16) * (LEAD // 128)
    vmem = pl.BlockSpec(memory_space=pltpu.VMEM)
    dma = pltpu.SemaphoreType.DMA
    updated, norm = pl.pallas_call(
        functools.partial(kernel, (nx, ny)),
        out_shape=(
            jax.ShapeDtypeStruct((blocks, rows, cols), jnp.bfloat16),
            jax.ShapeDtypeStruct((128,), jnp.float32),
        ),
        in_specs=[pl.BlockSpec(memory_space=pltpu.HBM)] * 7,
        out_specs=(vmem, vmem),
        scratch_shapes=[
            pltpu.SMEM(occ_pairs.shape, jnp.int32),
            pltpu.SMEM(vir_pairs.shape, jnp.int32),
            pltpu.VMEM(amplitudes.shape, amplitudes.dtype),
            pltpu.VMEM(hole_ints.shape, hole_ints.dtype),
            pltpu.VMEM(occ_energy.shape, jnp.float32),
            pltpu.VMEM(vir_energy.shape, jnp.float32),
            pltpu.VMEM((2, rows, cols), jnp.bfloat16),
            pltpu.VMEM((2, cols, cols), jnp.bfloat16),
            pltpu.VMEM((2, 2, lead + 1, 8, 128), jnp.int16),
            pltpu.VMEM((2, 2, lead + 1, 8, 128), jnp.int16),
            pltpu.VMEM((2, 2, tiles - lead, 8, 128), jnp.int16),
            pltpu.VMEM((2, 2, tiles - lead, 8, 128), jnp.int16),
            pltpu.VMEM((2, rows, 2 * cols), jnp.bfloat16),
            pltpu.VMEM((2, 4, 2 * cols, 4 * cols), jnp.bfloat16),
            pltpu.VMEM((2, 4, rows, 4 * cols), jnp.float32),
            pltpu.VMEM((2, rows, cols), jnp.float32),
            pltpu.VMEM((2, rows, cols), jnp.float32),
            pltpu.VMEM((2, 4, 6, tiles, 8, 128), jnp.int16),
            pltpu.VMEM((2, 4, 6, tiles, 8, 128), jnp.int16),
            pltpu.VMEM((2, 6, tiles, 8, 128), jnp.int16),
            pltpu.VMEM((2, 6, tiles, 8, 128), jnp.int16),
            pltpu.VMEM((2, 128), jnp.float32),
            pltpu.VMEM((ny * nv - 1, 2, 128), jnp.float32),
            dma((7,)),
            dma((2, 2)),
            dma((2,)),
            dma((2,)),
            dma((2,)),
            dma((2, 2, 2)),
            dma,
            dma((2,)),
            dma((4,)),
            dma((2, 8)),
            dma((4,)),
            dma((2, 9)),
            dma,
            dma((2, 4)),
            dma((2, 6)),
            dma,
            dma,
        ],
        compiler_params=pltpu.CompilerParams(
            collective_id=0, has_side_effects=True, vmem_limit_bytes=55_500_000
        ),
    )(
        *(
            pltpu.with_memory_space_constraint(array, pltpu.HBM)
            for array in (occ_pairs, vir_pairs, amplitudes, hole_ints, occ_energy, vir_energy, ladder_ints)
        )
    )
    return updated, norm[:2]


def solution(mesh):
    in_specs = (
        P("irrep", None, ("occ", "vir")),
        P("irrep", ("occ", "vir"), None),
        P("irrep", None, None),
        P("irrep", None),
        P("irrep", ("occ", "vir")),
        P(),
        P(),
    )
    out_specs = (P("irrep", None, ("occ", "vir")), P("irrep"))
    return jax.shard_map(body, mesh=mesh, in_specs=in_specs, out_specs=out_specs, check_vma=False)
```

time: 58.8 us -> 58.1 us (0.988)
  Pallas kernels: 56.7 us -> 56.1 us
    slice x1 -> x0, local copies, waits for them, and re-layouts: 0.63 us -> none  [body(): return (updated, norm[:, 0])]
    unnamed x1 -> x2, local copies, waits for them, and re-layouts: 0.78 us -> 1.29 us
where the time goes in v3:
time: 58.1 us; the launch traced here: 58 us
  Pallas kernels  56.1 us (97%)
  local copies, waits for them, and re-layouts  1.29 us (2%)
  between operations  0.64 us (1%)
    pallas_call x1, Pallas kernels, body(): pl.pallas_call(functools.partial(kernel, (nx, ny)), out_shape=(jax.ShapeD...  56.1 us
    unnamed x2, local copies, waits for them, and re-layouts  1.29 us

profile of v3, /device:TPU:1, one launch (start us, length us, event | category | flops | bytes accessed | tf_op | source)
XLA Modules:
  0.0 58.0 jit_solution(14334456261235578741)
XLA Ops:
  0.6 56.1 %shard_map.86 = (bf16[2,320,384]{2,1,0:T(8,128)(2,1)S(1)}, f32[128]{0:T(128)S(1)}) custom-call(s32[8]{0:T(128)} %occ_pairs_hbm.1, s32[8]{0:T(128)} %vir_pairs_hbm.1, bf16[2,320,384]{2,1,0:T(8,128)(2,1)} %amp_hbm.1, bf16[2,320,320]{2,1,0:T(8,128)(2,1)} %hole_hbm.1, f32[2,320]{1,0:T(2,128)} %occ_e_hbm.1, f32[2,384]{1,0:T(2,128)} %vir_e_hbm.1, ...), custom_call_target="tpu_custom_call" | custom-call | tf_op jit(solution)/shard_map/pallas_call | solution.py:467
  56.7 0.8 %copy.11 = bf16[2,320,384]{2,1,0:T(8,128)(2,1)} copy(bf16[2,320,384]{2,1,0:T(8,128)(2,1)S(1)} %get-tuple-element.8) | data formatting | bytes 983040
  57.5 0.5 copy.12

commit v4 on v3

--- a/solution.py
+++ b/solution.py
@@ -165,11 +165,11 @@
         load(n).start()
     load_ladder(0)
     pl.semaphore_wait(barrier, len(neighbours))
-    for b in range(2):
-        load(b).wait()
-        swap_amp(b).start()
     for n in range(2):
         for b in range(2):
+            if n == 0:
+                load(b).wait()
+                swap_amp(b).start()
             load_first(b, n).wait()
             swap_first(b, n).start()
     load_ladder(1)
@@ -277,10 +277,10 @@
         )
 
     def stage_first():
-        for b in range(2):
-            amplitudes(b)
         for n in range(2):
             for b in range(2):
+                if n == 0:
+                    amplitudes(b)
                 own = ladbuf.at[b, 0, pl.ds(0, cols), pl.ds(0, cols)]
                 if n == 0:
                     pltpu.make_async_copy(own, own, mine_s.at[b]).wait()

time: 58.1 us -> 57.9 us (level)
  no operation moved by 1% of the time
where the time goes in v4:
time: 57.9 us; the launch traced here: 57.8 us
  Pallas kernels  55.9 us (97%)
  local copies, waits for them, and re-layouts  1.29 us (2%)
  between operations  0.64 us (1%)
    pallas_call x1, Pallas kernels, body(): pl.pallas_call(functools.partial(kernel, (nx, ny)), out_shape=(jax.ShapeD...  55.9 us
    unnamed x2, local copies, waits for them, and re-layouts  1.29 us

profile of v4, /device:TPU:1, one launch (start us, length us, event | category | flops | bytes accessed | tf_op | source)
XLA Modules:
  0.0 57.8 jit_solution(17943975352607161186)
XLA Ops:
  0.6 55.9 %shard_map.86 = (bf16[2,320,384]{2,1,0:T(8,128)(2,1)S(1)}, f32[128]{0:T(128)S(1)}) custom-call(s32[8]{0:T(128)} %occ_pairs_hbm.1, s32[8]{0:T(128)} %vir_pairs_hbm.1, bf16[2,320,384]{2,1,0:T(8,128)(2,1)} %amp_hbm.1, bf16[2,320,320]{2,1,0:T(8,128)(2,1)} %hole_hbm.1, f32[2,320]{1,0:T(2,128)} %occ_e_hbm.1, f32[2,384]{1,0:T(2,128)} %vir_e_hbm.1, ...), custom_call_target="tpu_custom_call" | custom-call | tf_op jit(solution)/shard_map/pallas_call | solution.py:467
  56.5 0.8 %copy.11 = bf16[2,320,384]{2,1,0:T(8,128)(2,1)} copy(bf16[2,320,384]{2,1,0:T(8,128)(2,1)S(1)} %get-tuple-element.8) | data formatting | bytes 983040
  57.3 0.5 copy.12

commit v5 on v4

--- a/solution.py
+++ b/solution.py
@@ -49,6 +49,10 @@
     gap_of,
     msg_out,
     msg_in,
+    near_out,
+    near_in,
+    last_out,
+    last_in,
     two_out,
     two_in,
     sq_mine,
@@ -65,8 +69,11 @@
     lad_r,
     one_s,
     one_r,
+    near_s,
+    near_r,
+    last_s,
+    last_r,
     two_s,
-    last_r,
     two_r,
     sq_s,
     sq_r,
@@ -128,7 +135,7 @@
         return pltpu.make_async_remote_copy(
             first.at[b, :, where],
             ladbuf.at[b, 0, pl.ds(cols, cols), where],
-            lad_s.at[0],
+            lad_s,
             lad_r.at[b, 0] if part_no == 0 else late_r.at[b],
             device_id=peer,
             device_id_type=MESH,
@@ -141,7 +148,7 @@
                 pltpu.make_async_remote_copy(
                     lad.at[b, :, columns(b, s, t, 1 - c)],
                     ladbuf.at[b, s, pl.ds(cols, cols), pl.ds(t * cols, cols)],
-                    lad_s.at[s],
+                    lad_s,
                     lad_r.at[b, 2 * s + u],
                     device_id=peer,
                     device_id_type=MESH,
@@ -209,24 +216,25 @@
         swap_amp(b).wait_recv()
         amat[b, :, pl.ds(cols, cols)] = masked(amp_peer[b], b, 1 - c).astype(jnp.bfloat16)
 
-    def encode(ref, message, blocks):
+    def encode(ref, message, blocks, second=None):
+        tiles = [(ref, k) for k in blocks] + ([(second, k) for k in blocks] if second else [])
         biggest = None
-        for k in blocks:
-            here = jnp.max(jnp.abs(ref(k)[...]).reshape(groups, 8, 128), axis=0)
+        for source, k in tiles:
+            here = jnp.max(jnp.abs(source(k)[...]).reshape(groups, 8, 128), axis=0)
             biggest = here if biggest is None else jnp.maximum(biggest, here)
         code = jnp.ceil(jnp.log2(jnp.maximum(biggest, TINY)) * STEPS_PER_OCTAVE) + 1.0
         up = jnp.exp2(code * (-1.0 / STEPS_PER_OCTAVE)) * CODE_RANGE
-        for n, k in enumerate(blocks):
-            steps = jnp.round(ref(k)[...].reshape(groups, 8, 128) * up[None])
+        for n, (source, k) in enumerate(tiles):
+            steps = jnp.round(source(k)[...].reshape(groups, 8, 128) * up[None])
             message[pl.ds(n * groups, groups)] = steps.astype(jnp.int32).astype(jnp.int16)
-        message[len(blocks) * groups] = code.astype(jnp.int32).astype(jnp.int16)
-
-    def decoded(message, blocks):
-        code = message[len(blocks) * groups].astype(jnp.int32).astype(jnp.float32)
+        message[len(tiles) * groups] = code.astype(jnp.int32).astype(jnp.int16)
+
+    def decoded(message, blocks, n=0, pieces=1):
+        code = message[pieces * len(blocks) * groups].astype(jnp.int32).astype(jnp.float32)
         down = jnp.exp2(code * (1.0 / STEPS_PER_OCTAVE)) * (1.0 / CODE_RANGE)
 
         def read(k):
-            at = pl.ds((k - blocks[0]) * groups, groups)
+            at = pl.ds((n * len(blocks) + k - blocks[0]) * groups, groups)
             steps = message[at].astype(jnp.int32).astype(jnp.float32)
             return (steps * down[None]).reshape(half, 128)
 
@@ -239,7 +247,7 @@
         return ref
 
     def add_into(ref, messages, blocks):
-        reads = [decoded(m, blocks) for m in messages]
+        reads = [decoded(m[0], blocks, *m[1:]) if isinstance(m, tuple) else decoded(m, blocks) for m in messages]
         for k in blocks:
             total = ref(k)[...]
             for read in reads:
@@ -247,12 +255,23 @@
             ref(k)[...] = total
 
     def send_one(b, s, m):
-        return pltpu.make_async_remote_copy(
-            msg_out.at[b, s, m],
-            msg_in.at[b, s, m],
-            one_s.at[s],
-            last_r.at[b, m - 2] if s == 3 and m > 1 else one_r.at[b, 2 * s - 2 + m if m < 2 else 6 + s],
+        at = (b, s - 1, m) if m < 2 else (b, m - 2)
+        return pltpu.make_async_remote_copy(
+            (msg_out if m < 2 else last_out).at[at],
+            (msg_in if m < 2 else last_in).at[at],
+            one_s if m < 2 else last_s,
+            (one_r if m < 2 else last_r).at[at],
             device_id=shifted(b, 1 - 2 * (m % 2)),
+            device_id_type=MESH,
+        )
+
+    def send_near(b, s, d):
+        return pltpu.make_async_remote_copy(
+            near_out.at[b, s, d],
+            near_in.at[b, s, d],
+            near_s,
+            near_r.at[b, s],
+            device_id=shifted(b, 1 - 2 * d),
             device_id_type=MESH,
         )
 
@@ -303,13 +322,14 @@
     def emit(b, s, u):
         for d in range(2):
             t, h = (0, d) if u == 0 else (1 + d, 1 - d)
-            encode(piece(b, s, t, h), msg_out.at[b, s, 2 * u + d], whole)
+            encode(piece(b, s, t, h), msg_out.at[b, s - 1, d] if u == 0 else last_out.at[b, d], whole)
             send_one(b, s, 2 * u + d).start()
 
     def stage_a(s, u):
         for b in range(2):
             products(b, s, u)
-            emit(b, s, u)
+            if u == 0:
+                emit(b, s, u)
 
     def stage_b(s):
         for b in range(2):
@@ -320,16 +340,19 @@
                         add_into(piece(b, s, 1 + d, d), [(far_in, rear_in)[n].at[b, d]], parts[n])
                 else:
                     send_one(b, s, d).wait_recv()
-                    add_into(piece(b, s, 1 + d, d), [msg_in.at[b, s, d]], whole)
-                encode(piece(b, s, 1 + d, d), msg_out.at[b, s, 4 + d], whole)
-                send_one(b, s, 4 + d).start()
+                    add_into(piece(b, s, 1 + d, d), [msg_in.at[b, s - 1, d]], whole)
+                if s == 3:
+                    encode(piece(b, s, 1 + d, d), last_out.at[b, 2 + d], whole)
+                    send_one(b, s, 4 + d).start()
+                else:
+                    encode(piece(b, s, 1 + d, 1 - d), near_out.at[b, s, d], whole, piece(b, s, 1 + d, d))
+                    send_near(b, s, d).start()
 
     def stage_c(s):
         for b in range(2):
-            rest = msg_in.at[b, s, pl.ds(2, 4)]
-            pltpu.make_async_copy(rest, rest, one_r.at[b, 6 + s]).wait()
+            pltpu.make_async_copy(near_in.at[b, s], near_in.at[b, s], near_r.at[b, s]).wait()
             for d in range(2):
-                add_into(piece(b, s, 3, d), [msg_in.at[b, s, m] for m in (4 + d, 3 - d)], whole)
+                add_into(piece(b, s, 3, d), [(near_in.at[b, s, d], 1, 2), (near_in.at[b, s, 1 - d], 0, 2)], whole)
 
     def two_first(m):
         at, h = ((0, 0), (0, 1), (1, 1), (2, 0))[m]
@@ -386,7 +409,7 @@
     totals = [None, None]
     def add_one(b, h, m):
         send_one(b, 3, m).wait_recv()
-        add_into(piece(b, 3, 3, h), [msg_in.at[b, 3, m]], whole)
+        add_into(piece(b, 3, 3, h), [last_in.at[b, m - 2]], whole)
 
     def add_two(b, h, m):
         send_two(b, m).wait_recv()
@@ -440,11 +463,10 @@
     pltpu.make_async_copy(two_out, two_out, two_s).wait()
     for n, lot in enumerate((far_out, rear_out)):
         pltpu.make_async_copy(lot, lot, far_s.at[n]).wait()
-    for s in range(4):
-        theirs = ladbuf.at[:, s, pl.ds(cols, cols), :]
-        pltpu.make_async_copy(theirs, theirs, lad_s.at[s]).wait()
-        sent = msg_out.at[:, s] if s else msg_out.at[:, s, pl.ds(2, 4)]
-        pltpu.make_async_copy(sent, sent, one_s.at[s]).wait()
+    theirs = ladbuf.at[:, :, pl.ds(cols, cols), :]
+    pltpu.make_async_copy(theirs, theirs, lad_s).wait()
+    for lot, sem in ((msg_out, one_s), (near_out, near_s), (last_out, last_s)):
+        pltpu.make_async_copy(lot, lot, sem).wait()
     pltpu.make_async_copy(sq_all, sq_all, sq_s).wait()
     pltpu.make_async_copy(sq_all, sq_all, sq_r).wait()
     total = jnp.sum(sq_all[...], axis=0) + sq_mine[...]
@@ -490,8 +512,12 @@
             pltpu.VMEM((2, 4, rows, 4 * cols), jnp.float32),
             pltpu.VMEM((2, rows, cols), jnp.float32),
             pltpu.VMEM((2, rows, cols), jnp.float32),
-            pltpu.VMEM((2, 4, 6, tiles, 8, 128), jnp.int16),
-            pltpu.VMEM((2, 4, 6, tiles, 8, 128), jnp.int16),
+            pltpu.VMEM((2, 3, 2, tiles, 8, 128), jnp.int16),
+            pltpu.VMEM((2, 3, 2, tiles, 8, 128), jnp.int16),
+            pltpu.VMEM((2, 3, 2, 2 * tiles - 1, 8, 128), jnp.int16),
+            pltpu.VMEM((2, 3, 2, 2 * tiles - 1, 8, 128), jnp.int16),
+            pltpu.VMEM((2, 4, tiles, 8, 128), jnp.int16),
+            pltpu.VMEM((2, 4, tiles, 8, 128), jnp.int16),
             pltpu.VMEM((2, 6, tiles, 8, 128), jnp.int16),
             pltpu.VMEM((2, 6, tiles, 8, 128), jnp.int16),
             pltpu.VMEM((2, 128), jnp.float32),
@@ -504,12 +530,15 @@
             dma((2, 2, 2)),
             dma,
             dma((2,)),
-            dma((4,)),
+            dma,
             dma((2, 8)),
-            dma((4,)),
-            dma((2, 9)),
+            dma,
+            dma((2, 3, 2)),
+            dma,
+            dma((2, 3)),
             dma,
             dma((2, 4)),
+            dma,
             dma((2, 6)),
             dma,
             dma,

time: 57.9 us -> 57.8 us (level)
  no operation moved by 1% of the time
where the time goes in v5:
time: 57.8 us; the launch traced here: 57.7 us
  Pallas kernels  55.7 us (96%)
  local copies, waits for them, and re-layouts  1.29 us (2%)
  between operations  0.64 us (1%)
    pallas_call x1, Pallas kernels, body(): pl.pallas_call(functools.partial(kernel, (nx, ny)), out_shape=(jax.ShapeD...  55.7 us
    unnamed x2, local copies, waits for them, and re-layouts  1.29 us

profile of v5, /device:TPU:1, one launch (start us, length us, event | category | flops | bytes accessed | tf_op | source)
XLA Modules:
  0.0 57.7 jit_solution(4193539673146227592)
XLA Ops:
  0.6 55.7 %shard_map.86 = (bf16[2,320,384]{2,1,0:T(8,128)(2,1)S(1)}, f32[128]{0:T(128)S(1)}) custom-call(s32[8]{0:T(128)} %occ_pairs_hbm.1, s32[8]{0:T(128)} %vir_pairs_hbm.1, bf16[2,320,384]{2,1,0:T(8,128)(2,1)} %amp_hbm.1, bf16[2,320,320]{2,1,0:T(8,128)(2,1)} %hole_hbm.1, f32[2,320]{1,0:T(2,128)} %occ_e_hbm.1, f32[2,384]{1,0:T(2,128)} %vir_e_hbm.1, ...), custom_call_target="tpu_custom_call" | custom-call | tf_op jit(solution)/shard_map/pallas_call | solution.py:489
  56.4 0.8 %copy.11 = bf16[2,320,384]{2,1,0:T(8,128)(2,1)} copy(bf16[2,320,384]{2,1,0:T(8,128)(2,1)S(1)} %get-tuple-element.8) | data formatting | bytes 983040
  57.2 0.5 copy.12

commit v6 on v5

--- a/solution.py
+++ b/solution.py
@@ -474,8 +474,8 @@
     counts = [(occ_pairs[z * 2 + b] * vir_pairs[z * 2 + b]).astype(jnp.float32) for b in range(2)]
     block = lax.broadcasted_iota(jnp.int32, (2, 128), 0)
     norm = jnp.sqrt(total / jnp.where(block == 0, counts[0], counts[1]) + EPSILON)
-    lane = lax.broadcasted_iota(jnp.int32, (1, 128), 1)
-    norm_out[...] = jnp.where(lane == 0, norm[:1, :], norm[1:, :]).reshape(128)
+    for b in range(2):
+        norm_out[b] = norm[b, 0]
 
 
 def body(amplitudes, ladder_ints, hole_ints, occ_energy, vir_energy, occ_pairs, vir_pairs):
@@ -490,10 +490,10 @@
         functools.partial(kernel, (nx, ny)),
         out_shape=(
             jax.ShapeDtypeStruct((blocks, rows, cols), jnp.bfloat16),
-            jax.ShapeDtypeStruct((128,), jnp.float32),
+            jax.ShapeDtypeStruct((2,), jnp.float32),
         ),
         in_specs=[pl.BlockSpec(memory_space=pltpu.HBM)] * 7,
-        out_specs=(vmem, vmem),
+        out_specs=(vmem, pl.BlockSpec(memory_space=pltpu.SMEM)),
         scratch_shapes=[
             pltpu.SMEM(occ_pairs.shape, jnp.int32),
             pltpu.SMEM(vir_pairs.shape, jnp.int32),
@@ -552,7 +552,28 @@
             for array in (occ_pairs, vir_pairs, amplitudes, hole_ints, occ_energy, vir_energy, ladder_ints)
         )
     )
-    return updated, norm[:2]
+
+    def hand_over(updated_ref, norm_ref, updated_out, norm_out, sem):
+        copies = [
+            pltpu.make_async_copy(src, dst, sem.at[n])
+            for n, (src, dst) in enumerate(((updated_ref, updated_out), (norm_ref, norm_out)))
+        ]
+        for copy in copies:
+            copy.start()
+        for copy in copies:
+            copy.wait()
+
+    return pl.pallas_call(
+        hand_over,
+        out_shape=(
+            jax.ShapeDtypeStruct(updated.shape, updated.dtype),
+            jax.ShapeDtypeStruct(norm.shape, norm.dtype),
+        ),
+        in_specs=[vmem, vmem],
+        out_specs=(pl.BlockSpec(memory_space=pl.ANY),) * 2,
+        scratch_shapes=[dma((2,))],
+        compiler_params=pltpu.CompilerParams(vmem_limit_bytes=2_000_000),
+    )(updated, norm)
 
 
 def solution(mesh):

time: 57.8 us -> 57.9 us (level)
  Pallas kernels: 55.7 us -> 57.2 us
  local copies, waits for them, and re-layouts: 1.29 us -> 0 us
    unnamed x2 -> x0, local copies, waits for them, and re-layouts: 1.29 us -> none
    pallas_call x0 -> x1, Pallas kernels: none -> 0.8 us  [body(): pl.pallas_call(hand_over, out_shape=(jax.ShapeDtypeStruct(updated.shape,...]
    pallas_call x1, Pallas kernels: 55.7 us -> 56.4 us  [body(): pl.pallas_call(functools.partial(kernel, (nx, ny)), out_shape=(jax.ShapeD...]
where the time goes in v6:
time: 57.9 us; the launch traced here: 57.8 us
  Pallas kernels  57.2 us (99%)
  between operations  0.64 us (1%)
    pallas_call x1, Pallas kernels, body(): pl.pallas_call(functools.partial(kernel, (nx, ny)), out_shape=(jax.ShapeD...  56.4 us

profile of v6, /device:TPU:1, one launch (start us, length us, event | category | flops | bytes accessed | tf_op | source)
XLA Modules:
  0.0 57.8 jit_solution(1307485554396570284)
XLA Ops:
  0.6 56.4 %shard_map.86 = (bf16[2,320,384]{2,1,0:T(8,128)(2,1)S(1)}, f32[2]{0:T(128)S(1)}) custom-call(s32[8]{0:T(128)} %occ_pairs_hbm.1, s32[8]{0:T(128)} %vir_pairs_hbm.1, bf16[2,320,384]{2,1,0:T(8,128)(2,1)} %amp_hbm.1, bf16[2,320,320]{2,1,0:T(8,128)(2,1)} %hole_hbm.1, f32[2,320]{1,0:T(2,128)} %occ_e_hbm.1, f32[2,384]{1,0:T(2,128)} %vir_e_hbm.1, ...), custom_call_target="tpu_custom_call" | custom-call | tf_op jit(solution)/shard_map/pallas_call | solution.py:489
  57.0 0.8 %shard_map.87 = (bf16[2,320,384]{2,1,0:T(8,128)(2,1)}, f32[2]{0:T(128)}) custom-call(bf16[2,320,384]{2,1,0:T(8,128)(2,1)S(1)} %get-tuple-element.4.updated_ref, f32[2]{0:T(128)S(1)} %get-tuple-element.5.norm_ref), custom_call_target="tpu_custom_call" | custom-call | tf_op jit(solution)/shard_map/pallas_call | solution.py:566
